TPU v7x, 32 devices: a whole 2x2x4 slice. The times are simulated.
32 devices in a mesh: row: 4 (over y, x), col: 8 (over z, core).
Axes of the slice: x: 2, y: 2, z: 4, core: 2. Of those that a mesh axis runs over, the one named last changes fastest.
Arguments:
- pixels: bfloat16 [64, 16000, 144], P(None, ('row', 'col')), may hold values from 0.049804688 to 4
- match_filter: bfloat16 [16000, 2, 144], P(('row', 'col')), may hold values from -48 to 48
- tile_ranks: int32 [32, 64], P('row', 'col'), may hold values from 1 to 64
- column_order: int32 [64], replicated, may hold values from 0 to 63, each once
- right_factors: bfloat16 [32, 64, 64, 500], P('row', 'col'), may hold values from -0.25 to 0.25
- left_factors: bfloat16 [32, 64, 64, 500], P('row', 'col'), may hold values from -0.09375 to 0.09375
Outputs:
- commands: float32 [64, 16000], P(None, ('row', 'col'))
Inputs may be any that keep to these rules, and one draw needn't show every extreme that they name: `column_order`: every slope block is read by exactly one tile column.
All inputs are finite; a program needn't handle non-finite values.
Results may differ from a plain program's by a relative error of at most 0.0041.
Values may be sent and summed in bfloat16 or wider, within the bound.
No kernel may reach another device: no remote copies, remote signals or barrier semaphores. Data moves between devices by JAX's collectives and lax.ppermute only.
A program may use at most 128 MiB of HBM per device.

v0:
```python
import jax
import jax.numpy as jnp
from jax import lax
from jax.sharding import PartitionSpec as P


def centroid(frame_pixels, match_filter):
    flux = jnp.sum(frame_pixels.astype(jnp.float32), axis=2)
    raw = jnp.einsum("fsp,skp->fsk", frame_pixels, match_filter, preferred_element_type=jnp.float32)
    slopes = (raw / flux[:, :, None]).astype(jnp.bfloat16)
    return slopes.reshape(frame_pixels.shape[0], -1)


def route(slopes, order_mine, inverse, tile_width, col_count):
    frame_count = slopes.shape[0]
    block_count = slopes.shape[1] // tile_width
    own_blocks = jnp.transpose(slopes.reshape(frame_count, block_count, tile_width), (1, 0, 2))
    row_index = lax.axis_index("row")
    col_index = lax.axis_index("col")
    device_rank = row_index * col_count + col_index
    block_ids = device_rank * block_count + jnp.arange(block_count, dtype=jnp.int32)
    column_span = order_mine.shape[0]
    target = jnp.take(inverse, block_ids) // column_span
    selector = (jnp.arange(col_count, dtype=jnp.int32)[:, None] == target[None, :]).astype(
        jnp.bfloat16
    )
    outgoing = selector[:, :, None, None] * own_blocks[None]
    received = lax.all_to_all(outgoing, "col", split_axis=0, concat_axis=0, tiled=True)
    source_cols = jnp.arange(col_count, dtype=jnp.int32)
    source_ids = (
        (row_index * col_count + source_cols)[:, None] * block_count
        + jnp.arange(block_count, dtype=jnp.int32)[None, :]
    ).reshape(-1)
    tile_column = jnp.take(inverse, source_ids)
    valid = tile_column // column_span == col_index
    local_slot = tile_column - col_index * column_span
    placement = (
        (jnp.arange(column_span, dtype=jnp.int32)[:, None] == local_slot[None, :]) & valid[None, :]
    ).astype(jnp.bfloat16)
    flat_blocks = received.reshape(col_count * block_count, frame_count * tile_width)
    placed = jnp.dot(placement, flat_blocks, preferred_element_type=jnp.float32)
    summed = lax.psum(placed.astype(jnp.bfloat16), "row")
    return summed.reshape(column_span, frame_count, tile_width)


def shards(pixels, match_filter, tile_ranks, column_order, right_factors, left_factors):
    frame_count = pixels.shape[0]
    tile_width = right_factors.shape[3]
    rank_bound = right_factors.shape[2]
    column_span = right_factors.shape[1]
    col_count = lax.axis_size("col")
    col_index = lax.axis_index("col")
    order_mine = lax.dynamic_slice_in_dim(column_order, col_index * column_span, column_span)
    inverse = jnp.argsort(column_order, stable=True)
    slopes = centroid(pixels, match_filter)
    pieces = route(slopes, order_mine, inverse, tile_width, col_count)
    projection = jnp.einsum(
        "ijkt,jft->ijkf", right_factors, pieces, preferred_element_type=jnp.float32
    )
    component = lax.broadcasted_iota(jnp.int32, (1, 1, rank_bound), 2)
    keep = component < tile_ranks[:, :, None]
    projection = jnp.where(keep[:, :, :, None], projection, 0.0).astype(jnp.bfloat16)
    partial_cmd = jnp.einsum(
        "ijkf,ijka->fia", projection, left_factors, preferred_element_type=jnp.float32
    )
    partial_cmd = partial_cmd.reshape(frame_count, -1)
    return lax.psum_scatter(partial_cmd, "col", scatter_dimension=1, tiled=True)


def solution(mesh):
    in_specs = (
        P(None, ("row", "col"), None),
        P(("row", "col"), None, None),
        P("row", "col"),
        P(),
        P("row", "col", None, None),
        P("row", "col", None, None),
    )
    out_specs = P(None, ("row", "col"))
    return jax.shard_map(shards, mesh=mesh, in_specs=in_specs, out_specs=out_specs, check_vma=False)
```

profile of v0, /device:TPU:0, one launch (start us, length us, event | category | flops | bytes accessed | tf_op | source)
XLA Modules:
  0.0 210.0 jit_solution(3768200987633778871)
XLA Ops:
  6.5 24.2 %copy.15 = bf16[64,500,144]{2,0,1:T(8,128)(2,1)} copy(bf16[64,500,144]{1,2,0:T(8,128)(2,1)} %param.6) | data formatting | bytes 18432000 | tf_op args[0]
  30.8 0.0 copy-start.2
  30.8 0.0 copy-start
  30.8 6.0 %convert_reduce_fusion = f32[64,500]{1,0:T(8,128)S(1)} fusion(bf16[64,500,144]{1,2,0:T(8,128)(2,1)} %param.6), kind=kLoop, calls=%fused_computation.3 | loop fusion | flops 9184000 | bytes 9344000 | tf_op jit(solution)/shard_map/reduce_sum | solution.py:8
  36.8 0.0 copy-done.2
  36.9 2.0 sort.17
  38.9 0.6 gather_fusion.1
  39.6 0.0 copy-done
  39.6 0.9 copy.14
  40.4 0.1 copy.16
  40.6 10.0 %fusion.2 = bf16[64,500,2]{0,2,1:T(2,128)(2,1)S(1)} fusion(bf16[500,2,144]{2,1,0:T(2,128)(2,1)S(1)} %copy.14, bf16[64,500,144]{2,0,1:T(8,128)(2,1)} %copy.15, f32[64,500]{0,1:T(8,128)S(1)} %copy.16), kind=kOutput, calls=%fused_computation.9 | convolution fusion | flops 18560000 | bytes 9760000 | tf_op jit(solution)/shard_map/fsp,skp->fsk/dot_general | solution.py:9
  50.6 0.1 reshape_reshape.3
  50.7 0.2 copy.17
  50.8 1.1 broadcast_multiply_fusion
  52.0 0.0 copy-start.1
  52.0 6.5 %all-to-all-start = ((bf16[8,2,64,500]{3,2,1,0:T(8,128)(2,1)}), bf16[8,2,64,500]{3,2,1,0:T(8,128)(2,1)S(1)}, u32[]{:S(2)}, u32[]{:S(2)}) async-start(bf16[8,2,64,500]{3,2,1,0:T(8,128)(2,1)} %broadcast_multiply_fusion), calls=%async_computation | async-start | bytes 2097152 | tf_op jit(solution)/shard_map/all_to_all | solution.py:28
  58.5 0.0 all-reduce.4.cloned.1.call-start
  58.5 0.1 iota_add_fusion
  58.6 0.1 add.134
  58.7 0.1 add.132
  58.8 0.7 gather_fusion
  59.5 25.6 %all-to-all-done = bf16[8,2,64,500]{3,2,1,0:T(8,128)(2,1)S(1)} async-done(((bf16[8,2,64,500]{3,2,1,0:T(8,128)(2,1)}), bf16[8,2,64,500]{3,2,1,0:T(8,128)(2,1)S(1)}, u32[]{:S(2)}, u32[]{:S(2)}) %all-to-all-start) | async-done | bytes 1024032 | tf_op jit(solution)/shard_map/all_to_all | solution.py:28
  85.0 1.2 reshape.172
  86.3 0.3 convolution_convert_fusion
  86.5 1.9 reshape.173
  88.5 0.0 all-reduce.4.cloned.1.call-update
  88.5 0.2 all-reduce.6.cloned.1.call-start
  88.7 0.0 copy-done.1
  88.8 0.1 iota_compare_fusion
  88.8 44.2 %all-reduce.4.cloned.1.call-done = bf16[8,64,500]{2,1,0:T(8,128)(2,1)} async-done(((bf16[8,64,500]{2,1,0:T(8,128)(2,1)}), bf16[8,64,500]{2,1,0:T(8,128)(2,1)}) %all-reduce.4.cloned.1.call-update) | async-done | bytes 512016 | tf_op jit(solution)/shard_map/psum | solution.py:42
  133.0 6.5 %convolution_bitcast_fusion = f32[64,8,500]{2,0,1:T(8,128)S(1)} fusion(bf16[8,8,64,500]{3,2,1,0:T(8,128)(2,1)} %param.11, bf16[8,8,64,500]{3,2,1,0:T(8,128)(2,1)} %param.10, pred[8,8,64]{2,1,0:T(8,128)(4,1)S(1)} %iota_compare_fusion, bf16[8,64,500]{2,1,0:T(8,128)(2,1)} %all-reduce.4.cloned.1.call-done), kind=kOutput, calls=%fused_computation.6 | convolution fusion | flops 524812288 | bytes 9732096 | tf_op jit(solution)/shard_map/ijkf,ijka->fia/dot_general | solution.py:63
  139.5 0.0 copy-start.3
  139.5 0.6 copy.18
  140.1 1.9 reshape.174
  142.0 0.0 all-reduce.6.cloned.1.call-update
  142.0 0.0 copy-done.3
  142.1 0.6 dynamic-slice
  143.3 58.2 %all-reduce.6.cloned.1.call-done = f32[64,4000]{1,0:T(8,128)} async-done(((f32[64,4000]{1,0:T(8,128)}), f32[64,4000]{1,0:T(8,128)}) %all-reduce.6.cloned.1.call-update) | async-done | bytes 1024016
  201.5 1.7 constant_dynamic-slice_fusion
  (10 shorter events, 0.1 us)
Async XLA Ops:
  30.8 6.1 %copy-start.2 = (s32[64]{0:T(128)S(1)}, s32[64]{0:T(128)}, u32[]{:S(2)}) copy-start(s32[64]{0:T(128)} %param.9) | copy-start | bytes 772
  30.8 8.8 %copy-start = (bf16[500,2,144]{0,2,1:T(8,128)(2,1)S(1)}, bf16[500,2,144]{0,2,1:T(8,128)(2,1)}, u32[]{:S(2)}) copy-start(bf16[500,2,144]{0,2,1:T(8,128)(2,1)} %param.7) | copy-start | bytes 864004
  52.0 36.8 %copy-start.1 = (s32[8,8]{1,0:T(8,128)S(1)}, s32[8,8]{1,0:T(8,128)}, u32[]{:S(2)}) copy-start(s32[8,8]{1,0:T(8,128)} %param.8) | copy-start | bytes 772
  52.0 33.0 %all-to-all-start = ((bf16[8,2,64,500]{3,2,1,0:T(8,128)(2,1)}), bf16[8,2,64,500]{3,2,1,0:T(8,128)(2,1)S(1)}, u32[]{:S(2)}, u32[]{:S(2)}) async-start(bf16[8,2,64,500]{3,2,1,0:T(8,128)(2,1)} %broadcast_multiply_fusion), calls=%async_computation | async-start | bytes 2097152 | tf_op jit(solution)/shard_map/all_to_all | solution.py:28
  58.5 74.6 %all-reduce.4.cloned.1.call-start = ((), (), s32[]{:S(2)}) async-start(), calls=%async_computation.1 | async-start | bytes 1048576 | tf_op jit(solution)/shard_map/psum | solution.py:42
  88.5 113.0 %all-reduce.6.cloned.1.call-start = ((), (), s32[]{:S(2)}) async-start(), calls=%async_computation.2 | async-start | bytes 2097152
  139.5 2.6 %copy-start.3 = (u32[32]{0:T(128)S(1)}, u32[32]{0:T(128)}, u32[]{:S(2)}) copy-start(u32[32]{0:T(128)} %constant.70) | copy-start | bytes 388
Sparse Core Ops, SparseCore 0:
  88.6 44.3 all-reduce.3
  142.2 59.2 all-reduce.5
where the time goes:
time: 211 us; the launch traced here: 210 us
  waiting for transfers between devices  128 us (61%)
  local copies, waits for them, and re-layouts  34.9 us (17%)
  matrix products  16.8 us (8%)
  between operations  14.2 us (7%)
  other arithmetic  9.43 us (4%)
  starting transfers between devices  6.74 us (3%)
    unnamed x3, waiting for transfers between devices  58.2 us
    psum x1, waiting for transfers between devices, route(): summed = lax.psum(placed.astype(jnp.bfloat16), 'row')  44.2 us
    unnamed x12, local copies, waits for them, and re-layouts  27.4 us
    all_to_all x1, waiting for transfers between devices, route(): lax.all_to_all(outgoing, 'col', split_axis=0, concat_axis=0, tiled=True)  25.6 us
    dot_general x1, matrix products, centroid(): jnp.einsum('fsp,skp->fsk', frame_pixels, match_filter, preferred_element_...  10 us
    all_to_all x1, starting transfers between devices, route(): lax.all_to_all(outgoing, 'col', split_axis=0, concat_axis=0, tiled=True)  6.49 us
    dot_general x1, matrix products, shards(): jnp.einsum('ijkf,ijka->fia', projection, left_factors, preferred_element_...  6.47 us
    reduce_sum x1, other arithmetic, centroid(): flux = jnp.sum(frame_pixels.astype(jnp.float32), axis=2)  6.03 us
  transfers between devices with their start and end apart: 3, of which 3 were waited for; matrix products, arithmetic and copies ran while one was open for 1% of the time, Pallas kernels for 0%

commit v1 on v0

v1 whole, which is shorter than its diff:
```python
import functools

import jax
import jax.numpy as jnp
from jax import lax
from jax.experimental import pallas as pl
from jax.experimental.pallas import tpu as pltpu
from jax.sharding import PartitionSpec as P

F32 = jnp.float32
BF16 = jnp.bfloat16


def centroid_kernel(pix_ref, mf_ref, out_ref, filt, xs, ys, *, per_step, block_count, tile_width, group):
    step = pl.program_id(0)
    pixel_count, width = pix_ref.shape[1], pix_ref.shape[2]
    lanes = filt.shape[2]

    @pl.when(step == 0)
    def _():
        for k in range(2):
            filt[k, :, 0:width] = mf_ref[k].astype(F32)

    rows = 8
    for f0 in range(0, per_step, group):
        for lane in range(0, lanes, 128):
            w = min(128, width - lane)
            cols = slice(lane, lane + w)
            flux = [jnp.zeros((rows, w), F32) for _ in range(group)]
            sx = [jnp.zeros((rows, w), F32) for _ in range(group)]
            sy = [jnp.zeros((rows, w), F32) for _ in range(group)]
            for p in range(0, pixel_count, rows):
                m0 = filt[0, p : p + rows, cols]
                m1 = filt[1, p : p + rows, cols]
                for f in range(group):
                    v = pix_ref[f0 + f, p : p + rows, cols].astype(F32)
                    flux[f] = flux[f] + v
                    sx[f] = sx[f] + v * m0
                    sy[f] = sy[f] + v * m1
            fl = jnp.concatenate([jnp.sum(a, axis=0, keepdims=True) for a in flux], axis=0)
            vx = jnp.concatenate([jnp.sum(a, axis=0, keepdims=True) for a in sx], axis=0)
            vy = jnp.concatenate([jnp.sum(a, axis=0, keepdims=True) for a in sy], axis=0)
            at = pl.ds(pl.multiple_of(step * per_step + f0, group), group)
            xs[at, cols] = vx / fl
            ys[at, cols] = vy / fl

    @pl.when(step == pl.num_programs(0) - 1)
    def _():
        r = lax.broadcasted_iota(jnp.int32, (256, 256), 0)
        c = lax.broadcasted_iota(jnp.int32, (256, 256), 1)
        weave = (c == jnp.where(r < 128, 2 * r, 2 * (r - 128) + 1)).astype(BF16)
        lane_ok = lax.broadcasted_iota(jnp.int32, xs.shape, 1) < width
        x = jnp.where(lane_ok, xs[...], 0.0).astype(BF16)
        y = jnp.where(lane_ok, ys[...], 0.0).astype(BF16)
        parts = []
        for lane in range(0, lanes, 128):
            both = jnp.concatenate([x[:, lane : lane + 128], y[:, lane : lane + 128]], axis=1)
            parts.append(jnp.dot(both, weave, preferred_element_type=F32))
        woven = jnp.concatenate(parts, axis=1)
        chunk = out_ref.shape[1] // block_count
        for b in range(block_count):
            blk = woven[:, b * tile_width : (b + 1) * tile_width].astype(BF16)
            for q in range(out_ref.shape[0]):
                out_ref[q, b * chunk : (b + 1) * chunk, :] = blk[q * chunk : (q + 1) * chunk, :]


def centroid(pixels, match_filter, pieces, tile_width):
    frames, subaps, pixel_count = pixels.shape
    pix = jnp.transpose(pixels, (0, 2, 1))
    filt = jnp.transpose(match_filter, (1, 2, 0))
    per_step = 8
    lanes = -(-subaps // 128) * 128
    block_count = 2 * subaps // tile_width
    body = functools.partial(
        centroid_kernel, per_step=per_step, block_count=block_count, tile_width=tile_width, group=8
    )
    return pl.pallas_call(
        body,
        grid=(frames // per_step,),
        in_specs=[
            pl.BlockSpec((per_step, pixel_count, subaps), lambda s: (s, 0, 0)),
            pl.BlockSpec((2, pixel_count, subaps), lambda s: (0, 0, 0)),
        ],
        out_specs=pl.BlockSpec((pieces, block_count * frames // pieces, tile_width), lambda s: (0, 0, 0)),
        out_shape=jax.ShapeDtypeStruct((pieces, block_count * frames // pieces, tile_width), BF16),
        scratch_shapes=[
            pltpu.VMEM((2, pixel_count, lanes), F32),
            pltpu.VMEM((frames, lanes), F32),
            pltpu.VMEM((frames, lanes), F32),
        ],
        compiler_params=pltpu.CompilerParams(dimension_semantics=("arbitrary",)),
        name="centroid",
    )(pix, filt)


def select_kernel(order, in_ref, out_ref, wide, dest, *, block_count):
    chunk = in_ref.shape[1] // block_count
    wide[...] = in_ref[...].astype(F32)
    dests = out_ref.shape[0]
    span = out_ref.shape[1] // chunk
    for d in range(dests):
        for j in range(span):
            g = order[d * span + j]
            src = g // block_count
            b = g - src * block_count
            for f in range(chunk):
                dest[d, f * span + j : f * span + j + 1, :] = wide[src, pl.ds(b * chunk + f, 1), :]
    out_ref[...] = dest[...].astype(BF16)


def select(order, pieces, dests, block_count):
    rows = pieces.shape[0] * pieces.shape[1] // dests
    width = pieces.shape[2]
    return pl.pallas_call(
        functools.partial(select_kernel, block_count=block_count),
        in_specs=[pl.BlockSpec(memory_space=pltpu.SMEM), pl.BlockSpec(memory_space=pltpu.VMEM)],
        out_specs=pl.BlockSpec(memory_space=pltpu.VMEM),
        out_shape=jax.ShapeDtypeStruct((dests, rows, width), BF16),
        scratch_shapes=[pltpu.VMEM(pieces.shape, F32), pltpu.VMEM((dests, rows, width), F32)],
        name="select",
    )(order, pieces)


def spread_kernel(in_ref, out_ref, wide):
    span, frames, width = out_ref.shape
    for n in range(wide.shape[0]):
        w = min(128, width - 128 * n)
        wide[n, :, 0:w] = in_ref[:, 128 * n : 128 * n + w].astype(F32)
        for j in range(span):
            got = wide[n, pl.ds(j, frames, stride=span), :].astype(BF16)
            out_ref[j, :, 128 * n : 128 * n + w] = got[:, 0:w]


def spread(gathered, span):
    rows, width = gathered.shape
    return pl.pallas_call(
        spread_kernel,
        in_specs=[pl.BlockSpec(memory_space=pltpu.VMEM)],
        out_specs=pl.BlockSpec(memory_space=pltpu.VMEM),
        out_shape=jax.ShapeDtypeStruct((span, rows // span, width), BF16),
        scratch_shapes=[pltpu.VMEM((-(-width // 128), rows, 128), F32)],
        name="spread",
    )(gathered)


def tomo_kernel(index, ranks, picked_ref, right_ref, left_ref, out_ref, proj, *, count):
    rows, span, bound, _ = right_ref.shape
    frames = picked_ref.shape[1]
    component = lax.broadcasted_iota(jnp.int32, (bound, frames), 0)
    for m in range(count):
        i = index[m]
        for j in range(span):
            p = lax.dot_general(
                right_ref[i, j], picked_ref[j], (((1,), (1,)), ((), ())), preferred_element_type=F32
            )
            p = jnp.where(component < ranks[i, j], p, 0.0)
            proj[j * bound : (j + 1) * bound, :] = p.astype(BF16)
        left = left_ref[i].reshape(span * bound, left_ref.shape[3])
        out_ref[m] = lax.dot_general(
            proj[...], left, (((0,), (0,)), ((), ())), preferred_element_type=F32
        ).astype(out_ref.dtype)


def tomo(index, ranks, picked, right, left, dtype):
    count = index.shape[0]
    _, span, bound, width = right.shape
    frames = picked.shape[1]
    vmem = pl.BlockSpec(memory_space=pltpu.VMEM)
    smem = pl.BlockSpec(memory_space=pltpu.SMEM)
    return pl.pallas_call(
        functools.partial(tomo_kernel, count=count),
        in_specs=[smem, smem, vmem, vmem, vmem],
        out_specs=vmem,
        out_shape=jax.ShapeDtypeStruct((count, frames, left.shape[3]), dtype),
        scratch_shapes=[pltpu.VMEM((span * bound, frames), BF16)],
        name="tomo",
    )(index, ranks, picked, right, left)


def add_kernel(own_ref, other_ref, out_ref):
    out_ref[...] = own_ref[...] + other_ref[...].astype(F32)


def route_start(slopes, column_order, span, tile_width, col_count):
    frame_count = slopes.shape[1]
    block_count = slopes.shape[0]
    inverse = jnp.argsort(column_order, stable=True)
    row_index = lax.axis_index("row")
    col_index = lax.axis_index("col")
    device_rank = row_index * col_count + col_index
    block_ids = device_rank * block_count + jnp.arange(block_count, dtype=jnp.int32)
    target = jnp.take(inverse, block_ids) // span
    selector = (jnp.arange(col_count, dtype=jnp.int32)[:, None] == target[None, :]).astype(BF16)
    outgoing = selector[:, :, None, None] * slopes[None]
    received = lax.all_to_all(outgoing, "col", split_axis=0, concat_axis=0, tiled=True)
    source_ids = (
        (row_index * col_count + jnp.arange(col_count, dtype=jnp.int32))[:, None] * block_count
        + jnp.arange(block_count, dtype=jnp.int32)[None, :]
    ).reshape(-1)
    local_slot = jnp.take(inverse, source_ids) - col_index * span
    placement = (jnp.arange(span, dtype=jnp.int32)[:, None] == local_slot[None, :]).astype(BF16)
    flat_blocks = received.reshape(col_count * block_count, frame_count * tile_width)
    placed = jnp.dot(placement, flat_blocks, preferred_element_type=F32)
    return lax.psum(placed.astype(BF16), "row").reshape(span, frame_count, tile_width)


def shards(pixels, match_filter, tile_ranks, column_order, right_factors, left_factors):
    frames = pixels.shape[0]
    rows_mine, span, _, tile_width = right_factors.shape
    row_count = lax.axis_size("row")
    col_count = lax.axis_size("col")
    devices = row_count * col_count
    block_count = 2 * pixels.shape[1] // tile_width

    if frames % devices == 0:
        pieces = centroid(pixels, match_filter, devices, tile_width)
        pieces = lax.all_to_all(pieces, ("row", "col"), split_axis=0, concat_axis=0, tiled=True)
        outgoing = select(column_order, pieces, col_count, block_count)
        mine = lax.all_to_all(outgoing, "col", split_axis=0, concat_axis=0, tiled=True)
        gathered = lax.all_gather(mine, "row", axis=0, tiled=True)
        picked = spread(gathered.reshape(-1, tile_width), span)
    else:
        slopes = centroid(pixels, match_filter, 1, tile_width)
        slopes = slopes.reshape(block_count, frames, tile_width)
        picked = route_start(slopes, column_order, span, tile_width, col_count)

    chips = col_count // 2
    core = lax.axis_index("col") % 2
    chip = lax.axis_index("col") // 2
    actuators = rows_mine * left_factors.shape[3] // col_count
    if rows_mine == col_count:
        pairs = 2 * jnp.arange(chips, dtype=jnp.int32)
        theirs = tomo(pairs + (1 - core), tile_ranks, picked, right_factors, left_factors, BF16)
        received = lax.ppermute(theirs, "col", [(d, d ^ 1) for d in range(col_count)])
        ours = tomo(pairs + core, tile_ranks, picked, right_factors, left_factors, F32)
    else:
        every = tomo(jnp.arange(rows_mine, dtype=jnp.int32), tile_ranks, picked, right_factors, left_factors, F32)
        every = jnp.transpose(every, (1, 0, 2)).reshape(frames, chips, 2, actuators)
        every = jnp.transpose(every, (2, 1, 0, 3))
        theirs = lax.dynamic_index_in_dim(every, 1 - core, 0, keepdims=False).astype(BF16)
        received = lax.ppermute(theirs, "col", [(d, d ^ 1) for d in range(col_count)])
        ours = lax.dynamic_index_in_dim(every, core, 0, keepdims=False)
    total = ours + received.astype(F32)
    out = lax.dynamic_index_in_dim(total, chip, 0, keepdims=False)
    arrived = []
    for m in range(1, chips):
        piece = lax.dynamic_index_in_dim(total, (chip + m) % chips, 0, keepdims=False).astype(BF16)
        arrived.append(lax.ppermute(piece, "col", [(d, (d + 2 * m) % col_count) for d in range(col_count)]))
    for a in arrived:
        out = out + a.astype(F32)
    return out


def solution(mesh):
    in_specs = (
        P(None, ("row", "col"), None),
        P(("row", "col"), None, None),
        P("row", "col"),
        P(),
        P("row", "col", None, None),
        P("row", "col", None, None),
    )
    out_specs = P(None, ("row", "col"))
    return jax.shard_map(shards, mesh=mesh, in_specs=in_specs, out_specs=out_specs, check_vma=False)
```

time: 211 us -> 73.9 us (0.35)
  waiting for transfers between devices: 128 us -> 12.3 us
  local copies, waits for them, and re-layouts: 34.9 us -> 0.04 us
  blocking collectives: 0 us -> 25.6 us
  Pallas kernels: 0 us -> 25.3 us
  matrix products: 16.8 us -> 0 us
  between operations: 14.2 us -> 0.05 us
  other arithmetic: 9.43 us -> 2.89 us
    unnamed x3 -> x0, waiting for transfers between devices: 58.2 us -> none
    psum x1 -> x0, waiting for transfers between devices: 44.2 us -> none  [route(): summed = lax.psum(placed.astype(jnp.bfloat16), 'row')]
    unnamed x12 -> x0, local copies, waits for them, and re-layouts: 27.4 us -> none
    pallas_call x0 -> x5, Pallas kernels: none -> 25.3 us  [the longest x2 11.9 us: tomo(): pl.pallas_call(functools.partial(tomo_kernel, count=count), in_specs=[sme...]
    all_to_all x1, waiting for transfers between devices: 25.6 us -> 6.09 us  [shards(): lax.all_to_all(outgoing, 'col', split_axis=0, concat_axis=0, tiled=True)]
    dot_general x3 -> x0, matrix products: 16.8 us -> none  [the longest x1 10 us: centroid(): jnp.einsum('fsp,skp->fsk', frame_pixels, match_filter, preferred_element_...]
    all_to_all x0 -> x1, blocking collectives: none -> 15.6 us  [shards(): lax.all_to_all(pieces, ('row', 'col'), split_axis=0, concat_axis=0, tiled...]
    all_gather x0 -> x1, blocking collectives: none -> 9.97 us  [shards(): gathered = lax.all_gather(mine, 'row', axis=0, tiled=True)]
  transfers between devices with their start and end apart: 3 -> 5, of which waited for: 3 -> 3; matrix products, arithmetic and copies ran while one was open for 1% -> 1% of each run, Pallas kernels for 0% -> 8%
where the time goes in v1:
time: 73.9 us; the launch traced here: 73.4 us
  blocking collectives  25.6 us (35%)
  Pallas kernels  25.3 us (34%)
  waiting for transfers between devices  12.3 us (17%)
  starting transfers between devices  7.25 us (10%)
  other arithmetic  2.89 us (4%)
    all_to_all x1, blocking collectives, shards(): lax.all_to_all(pieces, ('row', 'col'), split_axis=0, concat_axis=0, tiled...  15.6 us
    pallas_call x2, Pallas kernels, tomo(): pl.pallas_call(functools.partial(tomo_kernel, count=count), in_specs=[sme...  11.9 us
    all_gather x1, blocking collectives, shards(): gathered = lax.all_gather(mine, 'row', axis=0, tiled=True)  9.97 us
    pallas_call x1, Pallas kernels, centroid(): pl.pallas_call(body, grid=(frames // per_step,), in_specs=[pl.BlockSpec((...  9.18 us
    ppermute x3, waiting for transfers between devices, shards(): lax.ppermute(piece, 'col', [(d, (d + 2 * m) % col_count) for d in range(c...  6.23 us
    all_to_all x1, waiting for transfers between devices, shards(): lax.all_to_all(outgoing, 'col', split_axis=0, concat_axis=0, tiled=True)  6.09 us
    ppermute x3, starting transfers between devices, shards(): lax.ppermute(piece, 'col', [(d, (d + 2 * m) % col_count) for d in range(c...  3.88 us
    all_to_all x1, starting transfers between devices, shards(): lax.all_to_all(outgoing, 'col', split_axis=0, concat_axis=0, tiled=True)  3.37 us
  transfers between devices with their start and end apart: 5, of which 3 were waited for; matrix products, arithmetic and copies ran while one was open for 1% of the time, Pallas kernels for 8%

profile of v1, /device:TPU:0, one launch (start us, length us, event | category | flops | bytes accessed | tf_op | source)
XLA Modules:
  0.0 73.4 jit_solution(217692210421400204)
XLA Ops:
  0.0 9.2 %centroid.1 = bf16[32,4,500]{2,1,0:T(4,128)(2,1)} custom-call(bf16[64,144,500]{2,1,0:T(8,128)(2,1)} %bitcast.15, bf16[2,144,500]{2,1,0:T(8,128)(2,1)} %bitcast.17), custom_call_target="tpu_custom_call" | custom-call | tf_op jit(solution)/shard_map/centroid/pallas_call | solution.py:77
  9.2 15.6 %all_to_all.10.in_ref = bf16[32,4,500]{2,1,0:T(4,128)(2,1)} all-to-all(bf16[32,4,500]{2,1,0:T(4,128)(2,1)} %centroid.1), channel_id=1, replica_groups=mesh['row'=4,'col'=8] {'row','col'}, dimensions={0} | all-to-all | bytes 256000 | tf_op jit(solution)/shard_map/all_to_all | solution.py:217
  24.8 2.2 %select.13 = bf16[8,16,500]{2,1,0:T(8,128)(2,1)} custom-call(s32[64]{0:T(128)} %order.1, bf16[32,4,500]{2,1,0:T(4,128)(2,1)} %all_to_all.10.in_ref), custom_call_target="tpu_custom_call" | custom-call | tf_op jit(solution)/shard_map/select/pallas_call | solution.py:114
  26.9 3.4 %all-to-all-start.1 = ((bf16[8,16,500]{2,1,0:T(8,128)(2,1)}), bf16[8,16,500]{2,1,0:T(8,128)(2,1)S(1)}, u32[]{:S(2)}, u32[]{:S(2)}) async-start(bf16[8,16,500]{2,1,0:T(8,128)(2,1)} %select.13), calls=%async_computation.1 | async-start | bytes 262144 | tf_op jit(solution)/shard_map/all_to_all | solution.py:219
  30.3 0.6 fusion.5.index
  30.9 6.1 %all-to-all-done.1 = bf16[8,16,500]{2,1,0:T(8,128)(2,1)S(1)} async-done(((bf16[8,16,500]{2,1,0:T(8,128)(2,1)}), bf16[8,16,500]{2,1,0:T(8,128)(2,1)S(1)}, u32[]{:S(2)}, u32[]{:S(2)}) %all-to-all-start.1) | async-done | bytes 128032 | tf_op jit(solution)/shard_map/all_to_all | solution.py:219
  37.0 10.0 %all_gather.3 = bf16[32,16,500]{2,1,0:T(8,128)(2,1)} all-gather(bf16[8,16,500]{2,1,0:T(8,128)(2,1)S(1)} %all-to-all-done.1), channel_id=1, replica_groups=mesh['row'=4,'col'=8] {'row'}, dimensions={0}, use_global_device_ids=true | all-gather | bytes 640000 | tf_op jit(solution)/shard_map/all_gather | solution.py:220
  47.0 2.1 %spread.1.picked_ref = bf16[8,64,500]{2,1,0:T(8,128)(2,1)} custom-call(bf16[512,500]{1,0:T(8,128)(2,1)} %bitcast.16), custom_call_target="tpu_custom_call" | custom-call | tf_op jit(solution)/shard_map/spread/pallas_call | solution.py:136
  49.1 5.9 %tomo.3 = bf16[4,64,500]{2,1,0:T(8,128)(2,1)} custom-call(s32[4]{0:T(128)} %fusion.5.index, s32[8,8]{1,0:T(8,128)} %ranks.3, bf16[8,64,500]{2,1,0:T(8,128)(2,1)} %spread.1.picked_ref, bf16[8,8,64,500]{3,2,1,0:T(8,128)(2,1)} %right_ref.3, bf16[8,8,64,500]{3,2,1,0:T(8,128)(2,1)} %left_ref.3), custom_call_target="tpu_custom_call" | custom-call | tf_op jit(solution)/shard_map/tomo/pallas_call | solution.py:170
  55.0 0.0 collective-permute-start
  55.0 0.5 fusion.6.index
  55.5 6.0 %tomo.2 = f32[4,64,500]{2,1,0:T(8,128)} custom-call(s32[4]{0:T(128)} %fusion.6.index, s32[8,8]{1,0:T(8,128)} %ranks.3, bf16[8,64,500]{2,1,0:T(8,128)(2,1)} %spread.1.picked_ref, bf16[8,8,64,500]{3,2,1,0:T(8,128)(2,1)} %right_ref.3, bf16[8,8,64,500]{3,2,1,0:T(8,128)(2,1)} %left_ref.3), custom_call_target="tpu_custom_call" | custom-call | tf_op jit(solution)/shard_map/tomo/pallas_call | solution.py:170
  61.5 0.0 collective-permute-done
  61.5 1.1 %convert_add_fusion = f32[4,64,500]{2,1,0:T(8,128)S(1)} fusion(f32[4,64,500]{2,1,0:T(8,128)} %tomo.2, bf16[4,64,500]{2,1,0:T(8,128)(2,1)S(1)} %collective-permute-done), kind=kLoop, calls=%fused_computation | loop fusion | flops 256000 | bytes 1280000 | tf_op jit(solution)/shard_map/add | solution.py:243
  62.6 1.0 %collective-permute-start.1 = (bf16[64,500]{1,0:T(8,128)(2,1)S(1)}, bf16[64,500]{1,0:T(8,128)(2,1)S(1)}, u32[]{:S(2)}, u32[]{:S(2)}) collective-permute-start(bf16[64,500]{1,0:T(8,128)(2,1)S(1)} %get-tuple-element.5), channel_id=1, source_target_pairs={{0,2},{1,3},{2,4},{3,5},{4,6},{5,7},{6,0},{7,1},{8,10},{9,11},{10,... | collective-permute-start | bytes 192008 | tf_op jit(solution)/shard_map/ppermute | solution.py:248
  63.6 2.9 %collective-permute-start.3 = (bf16[64,500]{1,0:T(8,128)(2,1)S(1)}, bf16[64,500]{1,0:T(8,128)(2,1)S(1)}, u32[]{:S(2)}, u32[]{:S(2)}) collective-permute-start(bf16[64,500]{1,0:T(8,128)(2,1)S(1)} %get-tuple-element.6), channel_id=1, source_target_pairs={{0,6},{1,7},{2,0},{3,1},{4,2},{5,3},{6,4},{7,5},{8,14},{9,15},{10,... | collective-permute-start | bytes 192008 | tf_op jit(solution)/shard_map/ppermute | solution.py:248
  66.5 0.0 collective-permute-start.2
  66.5 2.9 %collective-permute-done.1 = bf16[64,500]{1,0:T(8,128)(2,1)S(1)} collective-permute-done((bf16[64,500]{1,0:T(8,128)(2,1)S(1)}, bf16[64,500]{1,0:T(8,128)(2,1)S(1)}, u32[]{:S(2)}, u32[]{:S(2)}) %collective-permute-start.1) | collective-permute-done | bytes 64032 | tf_op jit(solution)/shard_map/ppermute | solution.py:248
  69.4 0.0 collective-permute-done.3
  69.5 3.3 %collective-permute-done.2 = bf16[64,500]{1,0:T(8,128)(2,1)S(1)} collective-permute-done((bf16[64,500]{1,0:T(8,128)(2,1)S(1)}, bf16[64,500]{1,0:T(8,128)(2,1)S(1)}, u32[]{:S(2)}, u32[]{:S(2)}) %collective-permute-start.2) | collective-permute-done | bytes 64032 | tf_op jit(solution)/shard_map/ppermute | solution.py:248
  72.7 0.7 fusion.1
  (1 shorter events, 0.0 us)
Async XLA Ops:
  26.9 10.1 %all-to-all-start.1 = ((bf16[8,16,500]{2,1,0:T(8,128)(2,1)}), bf16[8,16,500]{2,1,0:T(8,128)(2,1)S(1)}, u32[]{:S(2)}, u32[]{:S(2)}) async-start(bf16[8,16,500]{2,1,0:T(8,128)(2,1)} %select.13), calls=%async_computation.1 | async-start | bytes 262144 | tf_op jit(solution)/shard_map/all_to_all | solution.py:219
  55.0 6.5 %collective-permute-start = (bf16[4,64,500]{2,1,0:T(8,128)(2,1)}, bf16[4,64,500]{2,1,0:T(8,128)(2,1)S(1)}, u32[]{:S(2)}, u32[]{:S(2)}) collective-permute-start(bf16[4,64,500]{2,1,0:T(8,128)(2,1)} %tomo.3), channel_id=1, source_target_pairs={{0,1},{1,0},{2,3},{3,2},{4,5},{5,4},{6,7},{7,6},{8,9},{9,8},{10,11... | collective-permute-start | bytes 768008 | tf_op jit(solution)/shard_map/ppermute | solution.py:234
  62.6 6.8 %collective-permute-start.1 = (bf16[64,500]{1,0:T(8,128)(2,1)S(1)}, bf16[64,500]{1,0:T(8,128)(2,1)S(1)}, u32[]{:S(2)}, u32[]{:S(2)}) collective-permute-start(bf16[64,500]{1,0:T(8,128)(2,1)S(1)} %get-tuple-element.5), channel_id=1, source_target_pairs={{0,2},{1,3},{2,4},{3,5},{4,6},{5,7},{6,0},{7,1},{8,10},{9,11},{10,... | collective-permute-start | bytes 192008 | tf_op jit(solution)/shard_map/ppermute | solution.py:248
  63.6 5.8 %collective-permute-start.3 = (bf16[64,500]{1,0:T(8,128)(2,1)S(1)}, bf16[64,500]{1,0:T(8,128)(2,1)S(1)}, u32[]{:S(2)}, u32[]{:S(2)}) collective-permute-start(bf16[64,500]{1,0:T(8,128)(2,1)S(1)} %get-tuple-element.6), channel_id=1, source_target_pairs={{0,6},{1,7},{2,0},{3,1},{4,2},{5,3},{6,4},{7,5},{8,14},{9,15},{10,... | collective-permute-start | bytes 192008 | tf_op jit(solution)/shard_map/ppermute | solution.py:248
  66.5 6.2 %collective-permute-start.2 = (bf16[64,500]{1,0:T(8,128)(2,1)S(1)}, bf16[64,500]{1,0:T(8,128)(2,1)S(1)}, u32[]{:S(2)}, u32[]{:S(2)}) collective-permute-start(bf16[64,500]{1,0:T(8,128)(2,1)S(1)} %get-tuple-element.7), channel_id=1, source_target_pairs={{0,4},{1,5},{2,6},{3,7},{4,0},{5,1},{6,2},{7,3},{8,12},{9,13},{10,... | collective-permute-start | bytes 192008 | tf_op jit(solution)/shard_map/ppermute | solution.py:248

commit v2 on v1

v2 whole, which is shorter than its diff:
```python
import functools

import jax
import jax.numpy as jnp
from jax import lax
from jax.experimental import pallas as pl
from jax.experimental.pallas import tpu as pltpu
from jax.sharding import PartitionSpec as P

F32 = jnp.float32
BF16 = jnp.bfloat16


def in_vmem(x):
    return pltpu.with_memory_space_constraint(x, pltpu.VMEM)


def in_hbm(x):
    return pltpu.with_memory_space_constraint(x, pltpu.HBM)


def limit(mib):
    return pltpu.CompilerParams(vmem_limit_bytes=mib << 20)


VMEM = pl.BlockSpec(memory_space=pltpu.VMEM)
SMEM = pl.BlockSpec(memory_space=pltpu.SMEM)
HBM = pl.BlockSpec(memory_space=pltpu.HBM)
GROUP = 8


def centroid_kernel(pix_hbm, mf_ref, out_ref, pix, filt, xs, ys, sems, *, block_count, tile_width):
    frames, pixel_count, width = pix.shape
    lanes = filt.shape[2]
    steps = frames // GROUP

    def fetch(step):
        at = pl.ds(step * GROUP, GROUP)
        return pltpu.make_async_copy(pix_hbm.at[at], pix.at[at], sems.at[step])

    for step in range(steps):
        fetch(step).start()
    for k in range(2):
        filt[k, :, 0:width] = mf_ref[k].astype(F32)

    rows = 8

    @pl.loop(0, steps)
    def _(step):
        fetch(step).wait()
        f0 = pl.multiple_of(step * GROUP, GROUP)
        for lane in range(0, lanes, 128):
            w = min(128, width - lane)
            cols = slice(lane, lane + w)
            flux = [jnp.zeros((rows, w), F32) for _ in range(GROUP)]
            sx = [jnp.zeros((rows, w), F32) for _ in range(GROUP)]
            sy = [jnp.zeros((rows, w), F32) for _ in range(GROUP)]
            for p in range(0, pixel_count, rows):
                m0 = filt[0, p : p + rows, cols]
                m1 = filt[1, p : p + rows, cols]
                for f in range(GROUP):
                    v = pix[f0 + f, p : p + rows, cols].astype(F32)
                    flux[f] = flux[f] + v
                    sx[f] = sx[f] + v * m0
                    sy[f] = sy[f] + v * m1
            fl = jnp.concatenate([jnp.sum(a, axis=0, keepdims=True) for a in flux], axis=0)
            vx = jnp.concatenate([jnp.sum(a, axis=0, keepdims=True) for a in sx], axis=0)
            vy = jnp.concatenate([jnp.sum(a, axis=0, keepdims=True) for a in sy], axis=0)
            xs[pl.ds(f0, GROUP), cols] = vx / fl
            ys[pl.ds(f0, GROUP), cols] = vy / fl

    r = lax.broadcasted_iota(jnp.int32, (256, 256), 0)
    c = lax.broadcasted_iota(jnp.int32, (256, 256), 1)
    weave = (c == jnp.where(r < 128, 2 * r, 2 * (r - 128) + 1)).astype(BF16)
    lane_ok = lax.broadcasted_iota(jnp.int32, xs.shape, 1) < width
    x = jnp.where(lane_ok, xs[...], 0.0).astype(BF16)
    y = jnp.where(lane_ok, ys[...], 0.0).astype(BF16)
    parts = []
    for lane in range(0, lanes, 128):
        both = jnp.concatenate([x[:, lane : lane + 128], y[:, lane : lane + 128]], axis=1)
        parts.append(jnp.dot(both, weave, preferred_element_type=F32))
    woven = jnp.concatenate(parts, axis=1)
    chunk = out_ref.shape[1] // block_count
    for b in range(block_count):
        blk = woven[:, b * tile_width : (b + 1) * tile_width].astype(BF16)
        for q in range(out_ref.shape[0]):
            out_ref[q, b * chunk : (b + 1) * chunk, :] = blk[q * chunk : (q + 1) * chunk, :]


def centroid(pixels, match_filter, pieces, tile_width):
    frames, subaps, pixel_count = pixels.shape
    pix = jnp.transpose(pixels, (0, 2, 1))
    filt = jnp.transpose(match_filter, (1, 2, 0))
    lanes = -(-subaps // 128) * 128
    block_count = 2 * subaps // tile_width
    return pl.pallas_call(
        functools.partial(centroid_kernel, block_count=block_count, tile_width=tile_width),
        in_specs=[HBM, VMEM],
        out_specs=VMEM,
        out_shape=pltpu.VMEM((pieces, block_count * frames // pieces, tile_width), BF16),
        scratch_shapes=[
            pltpu.VMEM((frames, pixel_count, subaps), BF16),
            pltpu.VMEM((2, pixel_count, lanes), F32),
            pltpu.VMEM((frames, lanes), F32),
            pltpu.VMEM((frames, lanes), F32),
            pltpu.SemaphoreType.DMA((frames // GROUP,)),
        ],
        compiler_params=limit(16),
        name="centroid",
    )(in_hbm(pix), in_hbm(filt))


def select_kernel(order, in_ref, out_ref, wide, dest, *, block_count):
    chunk = in_ref.shape[1] // block_count
    wide[...] = in_ref[...].astype(F32)
    dests = out_ref.shape[0]
    span = out_ref.shape[1] // chunk
    for d in range(dests):
        for j in range(span):
            g = order[d * span + j]
            src = g // block_count
            b = g - src * block_count
            for f in range(chunk):
                dest[d, f * span + j : f * span + j + 1, :] = wide[src, pl.ds(b * chunk + f, 1), :]
    out_ref[...] = dest[...].astype(BF16)


def select(order, pieces, dests, block_count):
    rows = pieces.shape[0] * pieces.shape[1] // dests
    width = pieces.shape[2]
    return pl.pallas_call(
        functools.partial(select_kernel, block_count=block_count),
        in_specs=[SMEM, VMEM],
        out_specs=VMEM,
        out_shape=pltpu.VMEM((dests, rows, width), BF16),
        scratch_shapes=[pltpu.VMEM(pieces.shape, F32), pltpu.VMEM((dests, rows, width), F32)],
        compiler_params=limit(4),
        name="select",
    )(order, in_vmem(pieces))


def spread_kernel(in_ref, out_ref, wide):
    span, width, frames = out_ref.shape
    for n in range(wide.shape[0]):
        w = min(128, width - 128 * n)
        wide[n, :, 0:w] = in_ref[:, 128 * n : 128 * n + w].astype(F32)
        for j in range(span):
            got = jnp.transpose(wide[n, pl.ds(j, frames, stride=span), :]).astype(BF16)
            out_ref[j, 128 * n : 128 * n + w, :] = got[0:w]


def spread(gathered, span):
    rows, width = gathered.shape
    return pl.pallas_call(
        spread_kernel,
        in_specs=[VMEM],
        out_specs=VMEM,
        out_shape=pltpu.VMEM((span, width, rows // span), BF16),
        scratch_shapes=[pltpu.VMEM((-(-width // 128), rows, 128), F32)],
        compiler_params=limit(4),
        name="spread",
    )(in_vmem(gathered))


def tomo_kernel(ranks, picked_ref, right_ref, left_ref, out_ref, proj, *, pick):
    count = out_ref.shape[0]
    _, span, bound, _ = right_ref.shape
    frames = picked_ref.shape[2]
    component = lax.broadcasted_iota(jnp.int32, (bound, frames), 0)
    index = [pick(m) for m in range(count)]
    for j in range(span):
        right = jnp.concatenate([right_ref[i, j] for i in index], axis=0)
        p = jnp.dot(right, picked_ref[j], preferred_element_type=F32)
        for m, i in enumerate(index):
            q = jnp.where(component < ranks[i, j], p[m * bound : (m + 1) * bound], 0.0)
            proj[m, j * bound : (j + 1) * bound, :] = q.astype(BF16)
    for m, i in enumerate(index):
        left = left_ref[i].reshape(span * bound, left_ref.shape[3])
        out_ref[m] = lax.dot_general(
            proj[m], left, (((0,), (0,)), ((), ())), preferred_element_type=F32
        ).astype(out_ref.dtype)


def tomo(pick, count, ranks, picked, right, left, dtype):
    _, span, bound, _ = right.shape
    frames = picked.shape[2]
    return pl.pallas_call(
        functools.partial(tomo_kernel, pick=pick),
        in_specs=[SMEM, VMEM, VMEM, VMEM],
        out_specs=VMEM,
        out_shape=pltpu.VMEM((count, frames, left.shape[3]), dtype),
        scratch_shapes=[pltpu.VMEM((count, span * bound, frames), BF16)],
        compiler_params=limit(8),
        name="tomo",
    )(ranks, in_vmem(picked), in_vmem(right), in_vmem(left))


def own_core():
    return lax.rem(lax.axis_index("col"), 2)


def merge_kernel(own_ref, other_ref, out_ref, *send_refs):
    chips = own_ref.shape[0]
    chip = lax.div(lax.axis_index("col"), 2)
    out_ref[...] = own_ref[chip] + other_ref[chip].astype(F32)
    for m, send in enumerate(send_refs):
        at = lax.rem(chip + m + 1, chips)
        send[...] = (own_ref[at] + other_ref[at].astype(F32)).astype(BF16)


def merge(own, other):
    chips, frames, width = own.shape
    return pl.pallas_call(
        merge_kernel,
        in_specs=[VMEM, VMEM],
        out_specs=[VMEM] * chips,
        out_shape=[pltpu.VMEM((frames, width), F32)] + [pltpu.VMEM((frames, width), BF16)] * (chips - 1),
        compiler_params=limit(4),
        name="merge",
    )(in_vmem(own), in_vmem(other))


def route_start(slopes, column_order, span, tile_width, col_count):
    frame_count = slopes.shape[1]
    block_count = slopes.shape[0]
    inverse = jnp.argsort(column_order, stable=True)
    row_index = lax.axis_index("row")
    col_index = lax.axis_index("col")
    device_rank = row_index * col_count + col_index
    block_ids = device_rank * block_count + jnp.arange(block_count, dtype=jnp.int32)
    target = jnp.take(inverse, block_ids) // span
    selector = (jnp.arange(col_count, dtype=jnp.int32)[:, None] == target[None, :]).astype(BF16)
    outgoing = selector[:, :, None, None] * slopes[None]
    received = lax.all_to_all(outgoing, "col", split_axis=0, concat_axis=0, tiled=True)
    source_ids = (
        (row_index * col_count + jnp.arange(col_count, dtype=jnp.int32))[:, None] * block_count
        + jnp.arange(block_count, dtype=jnp.int32)[None, :]
    ).reshape(-1)
    local_slot = jnp.take(inverse, source_ids) - col_index * span
    placement = (jnp.arange(span, dtype=jnp.int32)[:, None] == local_slot[None, :]).astype(BF16)
    flat_blocks = received.reshape(col_count * block_count, frame_count * tile_width)
    placed = jnp.dot(placement, flat_blocks, preferred_element_type=F32)
    return lax.psum(placed.astype(BF16), "row").reshape(span, frame_count, tile_width)


def shards(pixels, match_filter, tile_ranks, column_order, right_factors, left_factors):
    frames = pixels.shape[0]
    rows_mine, span, _, tile_width = right_factors.shape
    row_count = lax.axis_size("row")
    col_count = lax.axis_size("col")
    devices = row_count * col_count
    block_count = 2 * pixels.shape[1] // tile_width

    if frames % devices == 0:
        pieces = centroid(pixels, match_filter, devices, tile_width)
        pieces = lax.all_to_all(pieces, ("row", "col"), split_axis=0, concat_axis=0, tiled=True)
        outgoing = select(column_order, pieces, col_count, block_count)
        mine = lax.all_to_all(outgoing, "col", split_axis=0, concat_axis=0, tiled=True)
        gathered = lax.all_gather(mine, "row", axis=0, tiled=True)
        picked = spread(gathered.reshape(-1, tile_width), span)
    else:
        slopes = centroid(pixels, match_filter, 1, tile_width)
        slopes = slopes.reshape(block_count, frames, tile_width)
        picked = route_start(slopes, column_order, span, tile_width, col_count)
        picked = jnp.transpose(picked, (0, 2, 1))

    chips = col_count // 2
    swap = [(d, d ^ 1) for d in range(col_count)]
    every = functools.partial(tomo, ranks=tile_ranks, picked=picked, right=right_factors, left=left_factors)
    if rows_mine == col_count:
        theirs = every(lambda m: 2 * m + 1 - own_core(), chips, dtype=BF16)
        received = lax.ppermute(theirs, "col", swap)
        ours = every(lambda m: 2 * m + own_core(), chips, dtype=F32)
    else:
        actuators = rows_mine * left_factors.shape[3] // col_count
        both = every(lambda m: m, rows_mine, dtype=F32)
        both = jnp.transpose(both, (1, 0, 2)).reshape(frames, chips, 2, actuators)
        both = jnp.transpose(both, (2, 1, 0, 3))
        theirs = lax.dynamic_index_in_dim(both, 1 - own_core(), 0, keepdims=False).astype(BF16)
        received = lax.ppermute(theirs, "col", swap)
        ours = lax.dynamic_index_in_dim(both, own_core(), 0, keepdims=False)
    out, *sends = merge(ours, received)
    for m, send in enumerate(sends):
        ahead = [(d, (d + 2 * (m + 1)) % col_count) for d in range(col_count)]
        out = out + lax.ppermute(send, "col", ahead).astype(F32)
    return out


def solution(mesh):
    in_specs = (
        P(None, ("row", "col"), None),
        P(("row", "col"), None, None),
        P("row", "col"),
        P(),
        P("row", "col", None, None),
        P("row", "col", None, None),
    )
    out_specs = P(None, ("row", "col"))
    return jax.shard_map(shards, mesh=mesh, in_specs=in_specs, out_specs=out_specs, check_vma=False)
```

time: 73.9 us -> 56.9 us (0.77)
  Pallas kernels: 25.3 us -> 12.8 us
  blocking collectives: 25.6 us -> 33.8 us
  waiting for transfers between devices: 12.3 us -> 5.37 us
  starting transfers between devices: 7.25 us -> 3.95 us
  other arithmetic: 2.89 us -> 0.69 us
    pallas_call x4 -> x5, Pallas kernels: 23.1 us -> 11.6 us  [the longest x1 7.65 us: centroid(): pl.pallas_call(functools.partial(centroid_kernel, block_count=block_count...]
    all_to_all x0 -> x1, blocking collectives: none -> 9.14 us  [shards(): lax.all_to_all(outgoing, 'col', split_axis=0, concat_axis=0, tiled=True)]
    all_to_all x1 -> x0, waiting for transfers between devices: 6.09 us -> none  [shards(): lax.all_to_all(outgoing, 'col', split_axis=0, concat_axis=0, tiled=True)]
    all_to_all x1 -> x0, starting transfers between devices: 3.37 us -> none  [shards(): lax.all_to_all(outgoing, 'col', split_axis=0, concat_axis=0, tiled=True)]
    add x4 -> x1, other arithmetic: 2.89 us -> 0.69 us  [shards(): out = out + lax.ppermute(send, 'col', ahead).astype(F32)]
    pallas_call x1, Pallas kernels: 2.15 us -> 1.13 us  [select(): pl.pallas_call(functools.partial(select_kernel, block_count=block_count),...]
    ppermute x4, waiting for transfers between devices: 6.23 us -> 5.37 us  [the longest x3 5.37 us: shards(): out = out + lax.ppermute(send, 'col', ahead).astype(F32)]
  transfers between devices with their start and end apart: 5 -> 4, of which waited for: 3 -> 2; matrix products, arithmetic and copies ran while one was open for 1% -> 0% of each run, Pallas kernels for 8% -> 3%
where the time goes in v2:
time: 56.9 us; the launch traced here: 56.7 us
  blocking collectives  33.8 us (59%)
  Pallas kernels  12.8 us (22%)
  waiting for transfers between devices  5.37 us (9%)
  starting transfers between devices  3.95 us (7%)
  other arithmetic  0.69 us (1%)
    all_to_all x1, blocking collectives, shards(): lax.all_to_all(pieces, ('row', 'col'), split_axis=0, concat_axis=0, tiled...  15.3 us
    all_gather x1, blocking collectives, shards(): gathered = lax.all_gather(mine, 'row', axis=0, tiled=True)  9.34 us
    all_to_all x1, blocking collectives, shards(): lax.all_to_all(outgoing, 'col', split_axis=0, concat_axis=0, tiled=True)  9.14 us
    pallas_call x1, Pallas kernels, centroid(): pl.pallas_call(functools.partial(centroid_kernel, block_count=block_count...  7.65 us
    ppermute x3, waiting for transfers between devices, shards(): out = out + lax.ppermute(send, 'col', ahead).astype(F32)  5.37 us
    ppermute x3, starting transfers between devices, shards(): out = out + lax.ppermute(send, 'col', ahead).astype(F32)  3.88 us
    pallas_call x2, Pallas kernels, tomo(): pl.pallas_call(functools.partial(tomo_kernel, pick=pick), in_specs=[SMEM,...  3.54 us
  transfers between devices with their start and end apart: 4, of which 2 were waited for; matrix products, arithmetic and copies ran while one was open for 0% of the time, Pallas kernels for 3%

profile of v2, /device:TPU:0, one launch (start us, length us, event | category | flops | bytes accessed | tf_op | source)
XLA Modules:
  0.0 56.7 jit_solution(4005581783052912471)
XLA Ops:
  0.0 0.0 copy-start.3
  0.0 0.0 copy-start
  0.0 0.0 copy-start.1
  0.0 0.0 copy-start.2
  0.0 7.7 %centroid.1 = bf16[32,4,500]{2,1,0:T(4,128)(2,1)S(1)} custom-call(bf16[64,144,500]{2,1,0:T(8,128)(2,1)} %bitcast.4, bf16[2,144,500]{2,1,0:T(8,128)(2,1)} %bitcast.5), custom_call_target="tpu_custom_call" | custom-call | tf_op jit(solution)/shard_map/centroid/pallas_call | solution.py:96
  7.7 15.3 %all_to_all.10.in_ref = bf16[32,4,500]{2,1,0:T(4,128)(2,1)S(1)} all-to-all(bf16[32,4,500]{2,1,0:T(4,128)(2,1)S(1)} %centroid.1), channel_id=1, replica_groups=mesh['row'=4,'col'=8] {'row','col'}, dimensions={0} | all-to-all | bytes 256000 | tf_op jit(solution)/shard_map/all_to_all | solution.py:256
  23.0 0.0 copy-done.3
  23.0 1.1 %select.1 = bf16[8,16,500]{2,1,0:T(8,128)(2,1)S(1)} custom-call(s32[64]{0:T(128)S(1)} %copy-done.3, bf16[32,4,500]{2,1,0:T(4,128)(2,1)S(1)} %all_to_all.10.in_ref), custom_call_target="tpu_custom_call" | custom-call | tf_op jit(solution)/shard_map/select/pallas_call | solution.py:131
  24.1 9.1 %all_to_all.11 = bf16[8,16,500]{2,1,0:T(8,128)(2,1)S(1)} all-to-all(bf16[8,16,500]{2,1,0:T(8,128)(2,1)S(1)} %select.1), channel_id=1, replica_groups=mesh['row'=4,'col'=8] {'col'}, dimensions={0} | all-to-all | bytes 256000 | tf_op jit(solution)/shard_map/all_to_all | solution.py:258
  33.3 9.3 %all_gather.3 = bf16[32,16,500]{2,1,0:T(8,128)(2,1)S(1)} all-gather(bf16[8,16,500]{2,1,0:T(8,128)(2,1)S(1)} %all_to_all.11), channel_id=1, replica_groups=mesh['row'=4,'col'=8] {'row'}, dimensions={0}, use_global_device_ids=true | all-gather | bytes 640000 | tf_op jit(solution)/shard_map/all_gather | solution.py:259
  42.6 0.4 spread.1.picked_ref
  43.0 0.0 copy-done
  43.0 0.0 copy-done.1
  43.0 0.0 copy-done.2
  43.0 1.8 %tomo.3 = bf16[4,64,500]{2,1,0:T(8,128)(2,1)S(1)} custom-call(s32[8,8]{1,0:T(8,128)S(1)} %copy-done.2, bf16[8,500,64]{2,1,0:T(8,128)(2,1)S(1)} %spread.1.picked_ref, bf16[8,8,64,500]{3,2,1,0:T(8,128)(2,1)S(1)} %copy-done, bf16[8,8,64,500]{3,2,1,0:T(8,128)(2,1)S(1)} %copy-done.1), custom_call_target="tpu_custom_call" | custom-call | tf_op jit(solution)/shard_map/tomo/pallas_call | solution.py:187
  44.8 0.1 collective-permute-start
  44.9 1.8 %tomo.2.own_ref = f32[4,64,500]{2,1,0:T(8,128)S(1)} custom-call(s32[8,8]{1,0:T(8,128)S(1)} %copy-done.2, bf16[8,500,64]{2,1,0:T(8,128)(2,1)S(1)} %spread.1.picked_ref, bf16[8,8,64,500]{3,2,1,0:T(8,128)(2,1)S(1)} %copy-done, bf16[8,8,64,500]{3,2,1,0:T(8,128)(2,1)S(1)} %copy-done.1), custom_call_target="tpu_custom_call" | custom-call | tf_op jit(solution)/shard_map/tomo/pallas_call | solution.py:187
  46.6 0.0 collective-permute-done.other_ref
  46.6 0.1 merge.1
  46.7 1.0 %collective-permute-start.1 = (bf16[64,500]{1,0:T(8,128)(2,1)S(1)}, bf16[64,500]{1,0:T(8,128)(2,1)S(1)}, u32[]{:S(2)}, u32[]{:S(2)}) collective-permute-start(bf16[64,500]{1,0:T(8,128)(2,1)S(1)} %get-tuple-element.10), channel_id=1, source_target_pairs={{0,2},{1,3},{2,4},{3,5},{4,6},{5,7},{6,0},{7,1},{8,10},{9,11},{10,... | collective-permute-start | bytes 192008 | tf_op jit(solution)/shard_map/ppermute | solution.py:285
  47.7 1.1 %collective-permute-start.2 = (bf16[64,500]{1,0:T(8,128)(2,1)S(1)}, bf16[64,500]{1,0:T(8,128)(2,1)S(1)}, u32[]{:S(2)}, u32[]{:S(2)}) collective-permute-start(bf16[64,500]{1,0:T(8,128)(2,1)S(1)} %get-tuple-element.11), channel_id=1, source_target_pairs={{0,4},{1,5},{2,6},{3,7},{4,0},{5,1},{6,2},{7,3},{8,12},{9,13},{10,... | collective-permute-start | bytes 192008 | tf_op jit(solution)/shard_map/ppermute | solution.py:285
  48.8 1.8 %collective-permute-start.3 = (bf16[64,500]{1,0:T(8,128)(2,1)S(1)}, bf16[64,500]{1,0:T(8,128)(2,1)S(1)}, u32[]{:S(2)}, u32[]{:S(2)}) collective-permute-start(bf16[64,500]{1,0:T(8,128)(2,1)S(1)} %get-tuple-element.12), channel_id=1, source_target_pairs={{0,6},{1,7},{2,0},{3,1},{4,2},{5,3},{6,4},{7,5},{8,14},{9,15},{10,... | collective-permute-start | bytes 192008 | tf_op jit(solution)/shard_map/ppermute | solution.py:285
  50.6 3.0 %collective-permute-done.1 = bf16[64,500]{1,0:T(8,128)(2,1)S(1)} collective-permute-done((bf16[64,500]{1,0:T(8,128)(2,1)S(1)}, bf16[64,500]{1,0:T(8,128)(2,1)S(1)}, u32[]{:S(2)}, u32[]{:S(2)}) %collective-permute-start.1) | collective-permute-done | bytes 64032 | tf_op jit(solution)/shard_map/ppermute | solution.py:285
  53.6 2.3 %collective-permute-done.2 = bf16[64,500]{1,0:T(8,128)(2,1)S(1)} collective-permute-done((bf16[64,500]{1,0:T(8,128)(2,1)S(1)}, bf16[64,500]{1,0:T(8,128)(2,1)S(1)}, u32[]{:S(2)}, u32[]{:S(2)}) %collective-permute-start.2) | collective-permute-done | bytes 64032 | tf_op jit(solution)/shard_map/ppermute | solution.py:285
  56.0 0.0 collective-permute-done.3
  56.0 0.7 %convert_add_fusion = f32[64,500]{1,0:T(8,128)} fusion(bf16[64,500]{1,0:T(8,128)(2,1)S(1)} %collective-permute-done.3, bf16[64,500]{1,0:T(8,128)(2,1)S(1)} %collective-permute-done.2, f32[64,500]{1,0:T(8,128)S(1)} %get-tuple-element.9, bf16[64,500]{1,0:T(8,128)(2,1)S(1)} %collective-permute-done.1), kind=kLoop, calls=%fused_computation | loop fusion | flops 192000 | bytes 448000 | tf_op jit(solution)/shard_map/add | solution.py:285
Async XLA Ops:
  0.0 23.0 %copy-start.3 = (s32[64]{0:T(128)S(1)}, s32[64]{0:T(128)}, u32[]{:S(2)}) copy-start(s32[64]{0:T(128)} %order.1) | copy-start | bytes 772
  0.0 43.0 %copy-start = (bf16[8,8,64,500]{3,2,1,0:T(8,128)(2,1)S(1)}, bf16[8,8,64,500]{3,2,1,0:T(8,128)(2,1)}, u32[]{:S(2)}) copy-start(bf16[8,8,64,500]{3,2,1,0:T(8,128)(2,1)} %right_ref.3) | copy-start | bytes 12288004
  0.0 43.0 %copy-start.1 = (bf16[8,8,64,500]{3,2,1,0:T(8,128)(2,1)S(1)}, bf16[8,8,64,500]{3,2,1,0:T(8,128)(2,1)}, u32[]{:S(2)}) copy-start(bf16[8,8,64,500]{3,2,1,0:T(8,128)(2,1)} %left_ref.3) | copy-start | bytes 12288004
  0.0 43.0 %copy-start.2 = (s32[8,8]{1,0:T(8,128)S(1)}, s32[8,8]{1,0:T(8,128)}, u32[]{:S(2)}) copy-start(s32[8,8]{1,0:T(8,128)} %ranks.3) | copy-start | bytes 772
  44.8 1.9 %collective-permute-start = (bf16[4,64,500]{2,1,0:T(8,128)(2,1)S(1)}, bf16[4,64,500]{2,1,0:T(8,128)(2,1)S(1)}, u32[]{:S(2)}, u32[]{:S(2)}) collective-permute-start(bf16[4,64,500]{2,1,0:T(8,128)(2,1)S(1)} %tomo.3), channel_id=1, source_target_pairs={{0,1},{1,0},{2,3},{3,2},{4,5},{5,4},{6,7},{7,6},{8,9},{9,8},{10,11... | collective-permute-start | bytes 768008 | tf_op jit(solution)/shard_map/ppermute | solution.py:272
  46.7 6.9 %collective-permute-start.1 = (bf16[64,500]{1,0:T(8,128)(2,1)S(1)}, bf16[64,500]{1,0:T(8,128)(2,1)S(1)}, u32[]{:S(2)}, u32[]{:S(2)}) collective-permute-start(bf16[64,500]{1,0:T(8,128)(2,1)S(1)} %get-tuple-element.10), channel_id=1, source_target_pairs={{0,2},{1,3},{2,4},{3,5},{4,6},{5,7},{6,0},{7,1},{8,10},{9,11},{10,... | collective-permute-start | bytes 192008 | tf_op jit(solution)/shard_map/ppermute | solution.py:285
  47.7 8.3 %collective-permute-start.2 = (bf16[64,500]{1,0:T(8,128)(2,1)S(1)}, bf16[64,500]{1,0:T(8,128)(2,1)S(1)}, u32[]{:S(2)}, u32[]{:S(2)}) collective-permute-start(bf16[64,500]{1,0:T(8,128)(2,1)S(1)} %get-tuple-element.11), channel_id=1, source_target_pairs={{0,4},{1,5},{2,6},{3,7},{4,0},{5,1},{6,2},{7,3},{8,12},{9,13},{10,... | collective-permute-start | bytes 192008 | tf_op jit(solution)/shard_map/ppermute | solution.py:285
  48.8 7.2 %collective-permute-start.3 = (bf16[64,500]{1,0:T(8,128)(2,1)S(1)}, bf16[64,500]{1,0:T(8,128)(2,1)S(1)}, u32[]{:S(2)}, u32[]{:S(2)}) collective-permute-start(bf16[64,500]{1,0:T(8,128)(2,1)S(1)} %get-tuple-element.12), channel_id=1, source_target_pairs={{0,6},{1,7},{2,0},{3,1},{4,2},{5,3},{6,4},{7,5},{8,14},{9,15},{10,... | collective-permute-start | bytes 192008 | tf_op jit(solution)/shard_map/ppermute | solution.py:285

commit v3 on v2

--- a/solution.py
+++ b/solution.py
@@ -24,24 +24,29 @@
 
 
 VMEM = pl.BlockSpec(memory_space=pltpu.VMEM)
-SMEM = pl.BlockSpec(memory_space=pltpu.SMEM)
 HBM = pl.BlockSpec(memory_space=pltpu.HBM)
 GROUP = 8
 
 
-def centroid_kernel(pix_hbm, mf_ref, out_ref, pix, filt, xs, ys, sems, *, block_count, tile_width):
-    frames, pixel_count, width = pix.shape
+def centroid_kernel(pix_hbm, mf_hbm, out_ref, pix, mf, filt, xs, ys, sems, *, block_count, tile_width):
+    chunk, pieces, pixel_count, width = pix_hbm.shape
     lanes = filt.shape[2]
-    steps = frames // GROUP
+    steps, inner, outer = pix.shape[:3]
 
     def fetch(step):
-        at = pl.ds(step * GROUP, GROUP)
-        return pltpu.make_async_copy(pix_hbm.at[at], pix.at[at], sems.at[step])
-
+        if inner == chunk:
+            source = pix_hbm.at[:, pl.ds(step * outer, outer)]
+        else:
+            source = pix_hbm.at[pl.ds(step * inner, inner), :]
+        return pltpu.make_async_copy(source, pix.at[step], sems.at[step])
+
+    fetch_mf = pltpu.make_async_copy(mf_hbm, mf, sems.at[steps])
+    fetch_mf.start()
     for step in range(steps):
         fetch(step).start()
+    fetch_mf.wait()
     for k in range(2):
-        filt[k, :, 0:width] = mf_ref[k].astype(F32)
+        filt[k, :, 0:width] = mf[k].astype(F32)
 
     rows = 8
 
@@ -59,7 +64,7 @@
                 m0 = filt[0, p : p + rows, cols]
                 m1 = filt[1, p : p + rows, cols]
                 for f in range(GROUP):
-                    v = pix[f0 + f, p : p + rows, cols].astype(F32)
+                    v = pix[step, f % inner, f // inner, p : p + rows, cols].astype(F32)
                     flux[f] = flux[f] + v
                     sx[f] = sx[f] + v * m0
                     sy[f] = sy[f] + v * m1
@@ -80,49 +85,56 @@
         both = jnp.concatenate([x[:, lane : lane + 128], y[:, lane : lane + 128]], axis=1)
         parts.append(jnp.dot(both, weave, preferred_element_type=F32))
     woven = jnp.concatenate(parts, axis=1)
-    chunk = out_ref.shape[1] // block_count
     for b in range(block_count):
         blk = woven[:, b * tile_width : (b + 1) * tile_width].astype(BF16)
-        for q in range(out_ref.shape[0]):
+        for q in range(pieces):
             out_ref[q, b * chunk : (b + 1) * chunk, :] = blk[q * chunk : (q + 1) * chunk, :]
 
 
 def centroid(pixels, match_filter, pieces, tile_width):
     frames, subaps, pixel_count = pixels.shape
-    pix = jnp.transpose(pixels, (0, 2, 1))
+    chunk = frames // pieces
+    inner = min(chunk, GROUP)
+    assert pieces == 1 or inner == chunk
+    pix = jnp.transpose(pixels, (0, 2, 1)).reshape(chunk, pieces, pixel_count, subaps)
     filt = jnp.transpose(match_filter, (1, 2, 0))
     lanes = -(-subaps // 128) * 128
     block_count = 2 * subaps // tile_width
     return pl.pallas_call(
         functools.partial(centroid_kernel, block_count=block_count, tile_width=tile_width),
-        in_specs=[HBM, VMEM],
+        in_specs=[HBM, HBM],
         out_specs=VMEM,
-        out_shape=pltpu.VMEM((pieces, block_count * frames // pieces, tile_width), BF16),
+        out_shape=pltpu.VMEM((pieces, block_count * chunk, tile_width), BF16),
         scratch_shapes=[
-            pltpu.VMEM((frames, pixel_count, subaps), BF16),
+            pltpu.VMEM((frames // GROUP, inner, GROUP // inner, pixel_count, subaps), BF16),
+            pltpu.VMEM((2, pixel_count, subaps), BF16),
             pltpu.VMEM((2, pixel_count, lanes), F32),
             pltpu.VMEM((frames, lanes), F32),
             pltpu.VMEM((frames, lanes), F32),
-            pltpu.SemaphoreType.DMA((frames // GROUP,)),
+            pltpu.SemaphoreType.DMA((frames // GROUP + 1,)),
         ],
         compiler_params=limit(16),
         name="centroid",
     )(in_hbm(pix), in_hbm(filt))
 
 
-def select_kernel(order, in_ref, out_ref, wide, dest, *, block_count):
-    chunk = in_ref.shape[1] // block_count
-    wide[...] = in_ref[...].astype(F32)
-    dests = out_ref.shape[0]
-    span = out_ref.shape[1] // chunk
+def select_kernel(order_ref, in_ref, out_ref, *, block_count):
+    sources, held, width = in_ref.shape
+    chunk = held // block_count
+    dests, rows, _ = out_ref.shape
+    span = rows // chunk
+    slots = order_ref.shape[1]
+    shape = (sources * held, chunk * slots)
+    row = lax.broadcasted_iota(jnp.int32, shape, 0)
+    wanted = jnp.concatenate([order_ref[...] * chunk + f for f in range(chunk)], axis=1)
+    pick = jnp.where(row == wanted, 1.0, 0.0).astype(BF16)
+    out = lax.dot_general(
+        pick, in_ref[...].reshape(sources * held, width), (((0,), (0,)), ((), ())), preferred_element_type=F32
+    ).astype(BF16)
     for d in range(dests):
-        for j in range(span):
-            g = order[d * span + j]
-            src = g // block_count
-            b = g - src * block_count
-            for f in range(chunk):
-                dest[d, f * span + j : f * span + j + 1, :] = wide[src, pl.ds(b * chunk + f, 1), :]
-    out_ref[...] = dest[...].astype(BF16)
+        for f in range(chunk):
+            at = f * slots + d * span
+            out_ref[d, f * span : (f + 1) * span, :] = out[at : at + span]
 
 
 def select(order, pieces, dests, block_count):
@@ -130,32 +142,33 @@
     width = pieces.shape[2]
     return pl.pallas_call(
         functools.partial(select_kernel, block_count=block_count),
-        in_specs=[SMEM, VMEM],
+        in_specs=[VMEM, VMEM],
         out_specs=VMEM,
         out_shape=pltpu.VMEM((dests, rows, width), BF16),
-        scratch_shapes=[pltpu.VMEM(pieces.shape, F32), pltpu.VMEM((dests, rows, width), F32)],
         compiler_params=limit(4),
         name="select",
-    )(order, in_vmem(pieces))
-
-
-def spread_kernel(in_ref, out_ref, wide):
-    span, width, frames = out_ref.shape
+    )(in_vmem(order.reshape(1, -1)), in_vmem(pieces))
+
+
+def spread_kernel(in_ref, out_ref, wide, *, pieces):
+    span, frames, width = out_ref.shape
+    chunk = frames // pieces
     for n in range(wide.shape[0]):
         w = min(128, width - 128 * n)
         wide[n, :, 0:w] = in_ref[:, 128 * n : 128 * n + w].astype(F32)
         for j in range(span):
-            got = jnp.transpose(wide[n, pl.ds(j, frames, stride=span), :]).astype(BF16)
-            out_ref[j, 128 * n : 128 * n + w, :] = got[0:w]
-
-
-def spread(gathered, span):
+            got = [wide[n, pl.ds(f * span + j, pieces, stride=span * chunk), :] for f in range(chunk)]
+            got = jnp.concatenate(got, axis=0).astype(BF16)
+            out_ref[j, :, 128 * n : 128 * n + w] = got[:, 0:w]
+
+
+def spread(gathered, span, pieces):
     rows, width = gathered.shape
     return pl.pallas_call(
-        spread_kernel,
+        functools.partial(spread_kernel, pieces=pieces),
         in_specs=[VMEM],
         out_specs=VMEM,
-        out_shape=pltpu.VMEM((span, width, rows // span), BF16),
+        out_shape=pltpu.VMEM((span, rows // span, width), BF16),
         scratch_shapes=[pltpu.VMEM((-(-width // 128), rows, 128), F32)],
         compiler_params=limit(4),
         name="spread",
@@ -165,14 +178,15 @@
 def tomo_kernel(ranks, picked_ref, right_ref, left_ref, out_ref, proj, *, pick):
     count = out_ref.shape[0]
     _, span, bound, _ = right_ref.shape
-    frames = picked_ref.shape[2]
+    frames = picked_ref.shape[1]
     component = lax.broadcasted_iota(jnp.int32, (bound, frames), 0)
     index = [pick(m) for m in range(count)]
+    limits = [ranks[pl.ds(i, 1), :] for i in index]
     for j in range(span):
         right = jnp.concatenate([right_ref[i, j] for i in index], axis=0)
-        p = jnp.dot(right, picked_ref[j], preferred_element_type=F32)
-        for m, i in enumerate(index):
-            q = jnp.where(component < ranks[i, j], p[m * bound : (m + 1) * bound], 0.0)
+        p = lax.dot_general(right, picked_ref[j], (((1,), (1,)), ((), ())), preferred_element_type=F32)
+        for m in range(count):
+            q = jnp.where(component < limits[m][:, j : j + 1], p[m * bound : (m + 1) * bound], 0.0)
             proj[m, j * bound : (j + 1) * bound, :] = q.astype(BF16)
     for m, i in enumerate(index):
         left = left_ref[i].reshape(span * bound, left_ref.shape[3])
@@ -183,38 +197,42 @@
 
 def tomo(pick, count, ranks, picked, right, left, dtype):
     _, span, bound, _ = right.shape
-    frames = picked.shape[2]
+    frames = picked.shape[1]
     return pl.pallas_call(
         functools.partial(tomo_kernel, pick=pick),
-        in_specs=[SMEM, VMEM, VMEM, VMEM],
+        in_specs=[VMEM, VMEM, VMEM, VMEM],
         out_specs=VMEM,
         out_shape=pltpu.VMEM((count, frames, left.shape[3]), dtype),
         scratch_shapes=[pltpu.VMEM((count, span * bound, frames), BF16)],
         compiler_params=limit(8),
         name="tomo",
-    )(ranks, in_vmem(picked), in_vmem(right), in_vmem(left))
+    )(in_vmem(ranks), in_vmem(picked), in_vmem(right), in_vmem(left))
 
 
 def own_core():
     return lax.rem(lax.axis_index("col"), 2)
 
 
-def merge_kernel(own_ref, other_ref, out_ref, *send_refs):
-    chips = own_ref.shape[0]
-    chip = lax.div(lax.axis_index("col"), 2)
-    out_ref[...] = own_ref[chip] + other_ref[chip].astype(F32)
+def own_chip():
+    return lax.div(lax.axis_index("col"), 2)
+
+
+def ahead(m, chips):
+    return lax.rem(own_chip() + m, chips)
+
+
+def merge_kernel(own_ref, other_ref, *send_refs):
     for m, send in enumerate(send_refs):
-        at = lax.rem(chip + m + 1, chips)
-        send[...] = (own_ref[at] + other_ref[at].astype(F32)).astype(BF16)
+        send[...] = (own_ref[m] + other_ref[m].astype(F32)).astype(BF16)
 
 
 def merge(own, other):
-    chips, frames, width = own.shape
+    count, frames, width = own.shape
     return pl.pallas_call(
         merge_kernel,
         in_specs=[VMEM, VMEM],
-        out_specs=[VMEM] * chips,
-        out_shape=[pltpu.VMEM((frames, width), F32)] + [pltpu.VMEM((frames, width), BF16)] * (chips - 1),
+        out_specs=[VMEM] * count,
+        out_shape=[pltpu.VMEM((frames, width), BF16)] * count,
         compiler_params=limit(4),
         name="merge",
     )(in_vmem(own), in_vmem(other))
@@ -257,32 +275,36 @@
         outgoing = select(column_order, pieces, col_count, block_count)
         mine = lax.all_to_all(outgoing, "col", split_axis=0, concat_axis=0, tiled=True)
         gathered = lax.all_gather(mine, "row", axis=0, tiled=True)
-        picked = spread(gathered.reshape(-1, tile_width), span)
+        picked = spread(gathered.reshape(-1, tile_width), span, devices)
     else:
         slopes = centroid(pixels, match_filter, 1, tile_width)
         slopes = slopes.reshape(block_count, frames, tile_width)
         picked = route_start(slopes, column_order, span, tile_width, col_count)
-        picked = jnp.transpose(picked, (0, 2, 1))
 
     chips = col_count // 2
+    order = [chips // 2] + [m for m in range(1, chips) if m != chips // 2] + [0]
     swap = [(d, d ^ 1) for d in range(col_count)]
     every = functools.partial(tomo, ranks=tile_ranks, picked=picked, right=right_factors, left=left_factors)
     if rows_mine == col_count:
-        theirs = every(lambda m: 2 * m + 1 - own_core(), chips, dtype=BF16)
+        theirs = every(lambda n: 2 * ahead(order[n], chips) + 1 - own_core(), chips, dtype=BF16)
         received = lax.ppermute(theirs, "col", swap)
-        ours = every(lambda m: 2 * m + own_core(), chips, dtype=F32)
+        ours = every(lambda n: 2 * ahead(order[n], chips) + own_core(), chips - 1, dtype=F32)
+        sends = merge(ours, received)
+        out = every(lambda n: 2 * own_chip() + own_core(), 1, dtype=F32)[0]
     else:
         actuators = rows_mine * left_factors.shape[3] // col_count
-        both = every(lambda m: m, rows_mine, dtype=F32)
+        both = every(lambda n: n, rows_mine, dtype=F32)
         both = jnp.transpose(both, (1, 0, 2)).reshape(frames, chips, 2, actuators)
         both = jnp.transpose(both, (2, 1, 0, 3))
+        both = jnp.take(both, jnp.stack([ahead(m, chips) for m in order]), axis=1)
         theirs = lax.dynamic_index_in_dim(both, 1 - own_core(), 0, keepdims=False).astype(BF16)
         received = lax.ppermute(theirs, "col", swap)
         ours = lax.dynamic_index_in_dim(both, own_core(), 0, keepdims=False)
-    out, *sends = merge(ours, received)
-    for m, send in enumerate(sends):
-        ahead = [(d, (d + 2 * (m + 1)) % col_count) for d in range(col_count)]
-        out = out + lax.ppermute(send, "col", ahead).astype(F32)
+        sends = merge(ours[: chips - 1], received)
+        out = ours[chips - 1]
+    out = out + received[chips - 1].astype(F32)
+    for m, send in zip(order, sends):
+        out = out + lax.ppermute(send, "col", [(d, (d + 2 * m) % col_count) for d in range(col_count)]).astype(F32)
     return out
 
 

time: 56.9 us -> 52.9 us (0.930)
  Pallas kernels: 12.8 us -> 9.59 us
  waiting for transfers between devices: 5.37 us -> 4.17 us
    ppermute x3, waiting for transfers between devices: 5.37 us -> 3.59 us  [shards(): lax.ppermute(send, 'col', [(d, (d + 2 * m) % col_count) for d in range(co...]
    pallas_call x1, Pallas kernels: 7.65 us -> 6.25 us  [centroid(): pl.pallas_call(functools.partial(centroid_kernel, block_count=block_count...]
    pallas_call x4 -> x5, Pallas kernels: 3.99 us -> 3.07 us  [the longest x3 2.61 us: tomo(): pl.pallas_call(functools.partial(tomo_kernel, pick=pick), in_specs=[VMEM,...]
    pallas_call x1, Pallas kernels: 1.13 us -> 0.28 us  [select(): pl.pallas_call(functools.partial(select_kernel, block_count=block_count),...]
    ppermute x1, waiting for transfers between devices: 0.01 us -> 0.58 us  [shards(): received = lax.ppermute(theirs, 'col', swap)]
where the time goes in v3:
time: 52.9 us; the launch traced here: 52.7 us
  blocking collectives  33.8 us (64%)
  Pallas kernels  9.59 us (18%)
  starting transfers between devices  4.35 us (8%)
  waiting for transfers between devices  4.17 us (8%)
  other arithmetic  0.7 us (1%)
    all_to_all x1, blocking collectives, shards(): lax.all_to_all(pieces, ('row', 'col'), split_axis=0, concat_axis=0, tiled...  15.3 us
    all_gather x1, blocking collectives, shards(): gathered = lax.all_gather(mine, 'row', axis=0, tiled=True)  9.34 us
    all_to_all x1, blocking collectives, shards(): lax.all_to_all(outgoing, 'col', split_axis=0, concat_axis=0, tiled=True)  9.14 us
    pallas_call x1, Pallas kernels, centroid(): pl.pallas_call(functools.partial(centroid_kernel, block_count=block_count...  6.25 us
    ppermute x3, starting transfers between devices, shards(): lax.ppermute(send, 'col', [(d, (d + 2 * m) % col_count) for d in range(co...  4.28 us
    ppermute x3, waiting for transfers between devices, shards(): lax.ppermute(send, 'col', [(d, (d + 2 * m) % col_count) for d in range(co...  3.59 us
    pallas_call x3, Pallas kernels, tomo(): pl.pallas_call(functools.partial(tomo_kernel, pick=pick), in_specs=[VMEM,...  2.61 us
  transfers between devices with their start and end apart: 4, of which 2 were waited for; matrix products, arithmetic and copies ran while one was open for 0% of the time, Pallas kernels for 3%

profile of v3, /device:TPU:0, one launch (start us, length us, event | category | flops | bytes accessed | tf_op | source)
XLA Modules:
  0.0 52.7 jit_solution(6779097742333393954)
XLA Ops:
  0.0 0.0 copy-start.3
  0.0 0.0 copy-start
  0.0 0.0 copy-start.1
  0.0 0.0 copy-start.2
  0.0 6.2 %centroid.1 = bf16[32,4,500]{2,1,0:T(4,128)(2,1)S(1)} custom-call(bf16[2,32,144,500]{3,2,1,0:T(8,128)(2,1)} %bitcast.14, bf16[2,144,500]{2,1,0:T(8,128)(2,1)} %bitcast.15), custom_call_target="tpu_custom_call" | custom-call | tf_op jit(solution)/shard_map/centroid/pallas_call | solution.py:103
  6.3 15.3 %all_to_all.10.in_ref = bf16[32,4,500]{2,1,0:T(4,128)(2,1)S(1)} all-to-all(bf16[32,4,500]{2,1,0:T(4,128)(2,1)S(1)} %centroid.1), channel_id=1, replica_groups=mesh['row'=4,'col'=8] {'row','col'}, dimensions={0} | all-to-all | bytes 256000 | tf_op jit(solution)/shard_map/all_to_all | solution.py:274
  21.6 0.0 copy-done.3
  21.6 0.3 select.1
  21.9 9.1 %all_to_all.11 = bf16[8,16,500]{2,1,0:T(8,128)(2,1)S(1)} all-to-all(bf16[8,16,500]{2,1,0:T(8,128)(2,1)S(1)} %select.1), channel_id=1, replica_groups=mesh['row'=4,'col'=8] {'col'}, dimensions={0} | all-to-all | bytes 256000 | tf_op jit(solution)/shard_map/all_to_all | solution.py:276
  31.0 9.3 %all_gather.3 = bf16[32,16,500]{2,1,0:T(8,128)(2,1)S(1)} all-gather(bf16[8,16,500]{2,1,0:T(8,128)(2,1)S(1)} %all_to_all.11), channel_id=1, replica_groups=mesh['row'=4,'col'=8] {'row'}, dimensions={0}, use_global_device_ids=true | all-gather | bytes 640000 | tf_op jit(solution)/shard_map/all_gather | solution.py:277
  40.3 0.4 spread.1.picked_ref
  40.8 0.0 copy-done
  40.8 0.0 copy-done.1
  40.8 0.0 copy-done.2
  40.8 1.2 %tomo.4 = bf16[4,64,500]{2,1,0:T(8,128)(2,1)S(1)} custom-call(s32[8,8]{1,0:T(8,128)S(1)} %copy-done.2, bf16[8,64,500]{2,1,0:T(8,128)(2,1)S(1)} %spread.1.picked_ref, bf16[8,8,64,500]{3,2,1,0:T(8,128)(2,1)S(1)} %copy-done, bf16[8,8,64,500]{3,2,1,0:T(8,128)(2,1)S(1)} %copy-done.1), custom_call_target="tpu_custom_call" | custom-call | tf_op jit(solution)/shard_map/tomo/pallas_call | solution.py:201
  42.0 0.1 collective-permute-start
  42.0 0.9 %tomo.5.own_ref = f32[3,64,500]{2,1,0:T(8,128)S(1)} custom-call(s32[8,8]{1,0:T(8,128)S(1)} %copy-done.2, bf16[8,64,500]{2,1,0:T(8,128)(2,1)S(1)} %spread.1.picked_ref, bf16[8,8,64,500]{3,2,1,0:T(8,128)(2,1)S(1)} %copy-done, bf16[8,8,64,500]{3,2,1,0:T(8,128)(2,1)S(1)} %copy-done.1), custom_call_target="tpu_custom_call" | custom-call | tf_op jit(solution)/shard_map/tomo/pallas_call | solution.py:201
  43.0 0.6 %collective-permute-done.other_ref = bf16[4,64,500]{2,1,0:T(8,128)(2,1)S(1)} collective-permute-done((bf16[4,64,500]{2,1,0:T(8,128)(2,1)S(1)}, bf16[4,64,500]{2,1,0:T(8,128)(2,1)S(1)}, u32[]{:S(2)}, u32[]{:S(2)}) %collective-permute-start) | collective-permute-done | bytes 256032 | tf_op jit(solution)/shard_map/ppermute | solution.py:290
  43.6 0.5 collective-permute-start.1
  44.1 1.6 %collective-permute-start.2 = (bf16[64,500]{1,0:T(8,128)(2,1)S(1)}, bf16[64,500]{1,0:T(8,128)(2,1)S(1)}, u32[]{:S(2)}, u32[]{:S(2)}) collective-permute-start(bf16[64,500]{1,0:T(8,128)(2,1)S(1)} %get-tuple-element.9), channel_id=1, source_target_pairs={{0,2},{1,3},{2,4},{3,5},{4,6},{5,7},{6,0},{7,1},{8,10},{9,11},{10,... | collective-permute-start | bytes 192008 | tf_op jit(solution)/shard_map/ppermute | solution.py:307
  45.7 2.2 %collective-permute-start.3 = (bf16[64,500]{1,0:T(8,128)(2,1)S(1)}, bf16[64,500]{1,0:T(8,128)(2,1)S(1)}, u32[]{:S(2)}, u32[]{:S(2)}) collective-permute-start(bf16[64,500]{1,0:T(8,128)(2,1)S(1)} %get-tuple-element.10), channel_id=1, source_target_pairs={{0,6},{1,7},{2,0},{3,1},{4,2},{5,3},{6,4},{7,5},{8,14},{9,15},{10,... | collective-permute-start | bytes 192008 | tf_op jit(solution)/shard_map/ppermute | solution.py:307
  47.9 0.5 tomo.3
  48.4 3.6 %collective-permute-done.1 = bf16[64,500]{1,0:T(8,128)(2,1)S(1)} collective-permute-done((bf16[64,500]{1,0:T(8,128)(2,1)S(1)}, bf16[64,500]{1,0:T(8,128)(2,1)S(1)}, u32[]{:S(2)}, u32[]{:S(2)}) %collective-permute-start.1) | collective-permute-done | bytes 64032 | tf_op jit(solution)/shard_map/ppermute | solution.py:307
  52.0 0.0 collective-permute-done.2
  52.0 0.0 collective-permute-done.3
  52.0 0.7 %fusion.1 = f32[64,500]{1,0:T(8,128)} fusion(bf16[64,500]{1,0:T(8,128)(2,1)S(1)} %collective-permute-done.3, bf16[64,500]{1,0:T(8,128)(2,1)S(1)} %collective-permute-done.2, bf16[64,500]{1,0:T(8,128)(2,1)S(1)} %collective-permute-done.1, f32[1,64,500]{2,1,0:T(8,128)S(1)} %tomo.3, bf16[4,64,500]{2,1,0:T(8,128)(2,1)S(1)} %collective-permute-done.other_ref), kind=kLoop, calls=%fused_computation.2 | loop fusion | flops 256000 | bytes 512000 | tf_op jit(solution)/shard_map/add | solution.py:307
  (1 shorter events, 0.0 us)
Async XLA Ops:
  0.0 21.6 %copy-start.3 = (s32[64]{0:T(128)S(1)}, s32[64]{0:T(128)}, u32[]{:S(2)}) copy-start(s32[64]{0:T(128)} %param.9) | copy-start | bytes 772
  0.0 40.8 %copy-start = (bf16[8,8,64,500]{3,2,1,0:T(8,128)(2,1)S(1)}, bf16[8,8,64,500]{3,2,1,0:T(8,128)(2,1)}, u32[]{:S(2)}) copy-start(bf16[8,8,64,500]{3,2,1,0:T(8,128)(2,1)} %right_ref.5) | copy-start | bytes 12288004
  0.0 40.8 %copy-start.1 = (bf16[8,8,64,500]{3,2,1,0:T(8,128)(2,1)S(1)}, bf16[8,8,64,500]{3,2,1,0:T(8,128)(2,1)}, u32[]{:S(2)}) copy-start(bf16[8,8,64,500]{3,2,1,0:T(8,128)(2,1)} %left_ref.5) | copy-start | bytes 12288004
  0.0 40.8 %copy-start.2 = (s32[8,8]{1,0:T(8,128)S(1)}, s32[8,8]{1,0:T(8,128)}, u32[]{:S(2)}) copy-start(s32[8,8]{1,0:T(8,128)} %ranks.5) | copy-start | bytes 772
  42.0 1.6 %collective-permute-start = (bf16[4,64,500]{2,1,0:T(8,128)(2,1)S(1)}, bf16[4,64,500]{2,1,0:T(8,128)(2,1)S(1)}, u32[]{:S(2)}, u32[]{:S(2)}) collective-permute-start(bf16[4,64,500]{2,1,0:T(8,128)(2,1)S(1)} %tomo.4), channel_id=1, source_target_pairs={{0,1},{1,0},{2,3},{3,2},{4,5},{5,4},{6,7},{7,6},{8,9},{9,8},{10,11... | collective-permute-start | bytes 768008 | tf_op jit(solution)/shard_map/ppermute | solution.py:290
  43.6 8.4 %collective-permute-start.1 = (bf16[64,500]{1,0:T(8,128)(2,1)S(1)}, bf16[64,500]{1,0:T(8,128)(2,1)S(1)}, u32[]{:S(2)}, u32[]{:S(2)}) collective-permute-start(bf16[64,500]{1,0:T(8,128)(2,1)S(1)} %get-tuple-element.8), channel_id=1, source_target_pairs={{0,4},{1,5},{2,6},{3,7},{4,0},{5,1},{6,2},{7,3},{8,12},{9,13},{10,... | collective-permute-start | bytes 192008 | tf_op jit(solution)/shard_map/ppermute | solution.py:307
  44.1 7.9 %collective-permute-start.2 = (bf16[64,500]{1,0:T(8,128)(2,1)S(1)}, bf16[64,500]{1,0:T(8,128)(2,1)S(1)}, u32[]{:S(2)}, u32[]{:S(2)}) collective-permute-start(bf16[64,500]{1,0:T(8,128)(2,1)S(1)} %get-tuple-element.9), channel_id=1, source_target_pairs={{0,2},{1,3},{2,4},{3,5},{4,6},{5,7},{6,0},{7,1},{8,10},{9,11},{10,... | collective-permute-start | bytes 192008 | tf_op jit(solution)/shard_map/ppermute | solution.py:307
  45.7 6.3 %collective-permute-start.3 = (bf16[64,500]{1,0:T(8,128)(2,1)S(1)}, bf16[64,500]{1,0:T(8,128)(2,1)S(1)}, u32[]{:S(2)}, u32[]{:S(2)}) collective-permute-start(bf16[64,500]{1,0:T(8,128)(2,1)S(1)} %get-tuple-element.10), channel_id=1, source_target_pairs={{0,6},{1,7},{2,0},{3,1},{4,2},{5,3},{6,4},{7,5},{8,14},{9,15},{10,... | collective-permute-start | bytes 192008 | tf_op jit(solution)/shard_map/ppermute | solution.py:307
